TPU v7x, 32 devices: a whole 2x2x4 slice. The times are simulated.
32 devices in a mesh: blk: 4 (over x, core), grp: 8 (over z, y).
Axes of the slice: x: 2, y: 2, z: 4, core: 2. Of those that a mesh axis runs over, the one named last changes fastest.
Arguments:
- text: bfloat16 [32, 512], P(('blk', 'grp')), may hold values from -20 to 20
- keys: bfloat16 [32, 196, 512], P(('blk', 'grp')), may hold values from -400 to 400
- values: bfloat16 [32, 196, 512], P(('blk', 'grp')), may hold values from -5 to 5
- pair_image: int32 [32], replicated, may hold values from 0 to 31, each once
Outputs:
- caption_loss: float32 [32], P(('blk', 'grp'))
- grad_text: float32 [32, 512], P(('blk', 'grp'))
- grad_keys: float32 [32, 196, 512], P(('blk', 'grp'))
- grad_values: float32 [32, 196, 512], P(('blk', 'grp'))
All inputs are finite; a program needn't handle non-finite values.
Results may differ from a plain program's by a relative error of at most 0.008.
Values may be sent and summed in bfloat16 or wider, within the bound.
A program may use at most 64 MiB of HBM per device.

v0:
```python
import jax
import jax.numpy as jnp
from jax import lax
from jax.sharding import PartitionSpec as P

HEADS = 8
EPS = 1e-06
LOGIT_SCALE = 10.0
LOGIT_BIAS = -1.0


def passed_along(block, axis, distance):
    devices = range(lax.axis_size(axis))
    route = [((i - distance) % len(devices), i) for i in devices]
    return lax.ppermute(block, axis, route)


def image_terms(block_text, normed, tnorm, pairs, image_id, keys_one, values_one):
    count = block_text.shape[0]
    width = block_text.shape[1]
    depth = width // HEADS
    queries = block_text.reshape(count, HEADS, depth)
    patch_keys = keys_one.reshape(-1, HEADS, depth)
    patch_values = values_one.reshape(-1, HEADS, depth)
    scores = jnp.einsum(
        "chd,phd->chp", queries, patch_keys, preferred_element_type=jnp.float32
    ) * depth ** (-0.5)
    weights = jax.nn.softmax(scores, axis=-1)
    attn = weights.astype(jnp.bfloat16)
    pooled = jnp.einsum(
        "chp,phd->chd", attn, patch_values, preferred_element_type=jnp.float32
    ).reshape(count, width)
    pnorm = lax.rsqrt(jnp.mean(pooled * pooled, -1, keepdims=True) + EPS)
    unit = pooled * pnorm
    cosine = jnp.mean(unit * normed, -1)
    logit = LOGIT_SCALE * cosine + LOGIT_BIAS
    label = jnp.where(pairs == image_id, 1.0, -1.0).astype(jnp.float32)
    loss = jax.nn.softplus(-label * logit)
    slope = -label * jax.nn.sigmoid(-label * logit)
    dcos = LOGIT_SCALE / width * slope[:, None]
    dunit = dcos * normed
    dnormed = dcos * unit
    dpool = pnorm * (dunit - unit * jnp.mean(dunit * unit, -1, keepdims=True))
    dout = dpool.astype(jnp.bfloat16).reshape(count, HEADS, depth)
    dattn = jnp.einsum("chd,phd->chp", dout, patch_values, preferred_element_type=jnp.float32)
    grad_v = jnp.einsum("chp,chd->phd", attn, dout, preferred_element_type=jnp.float32).reshape(
        -1, width
    )
    dscore = (
        weights * (dattn - jnp.sum(weights * dattn, -1, keepdims=True)) * depth ** (-0.5)
    ).astype(jnp.bfloat16)
    grad_q = jnp.einsum(
        "chp,phd->chd", dscore, patch_keys, preferred_element_type=jnp.float32
    ).reshape(count, width)
    grad_k = jnp.einsum(
        "chp,chd->phd", dscore, queries, preferred_element_type=jnp.float32
    ).reshape(-1, width)
    grad_x = grad_q + tnorm * (dnormed - normed * jnp.mean(dnormed * normed, -1, keepdims=True))
    return (loss, grad_x, grad_k, grad_v)


def pair_block(block_text, pair_image, first_caption, keys, values, first_image):
    count = block_text.shape[0]
    width = block_text.shape[1]
    text_wide = block_text.astype(jnp.float32)
    tnorm = lax.rsqrt(jnp.mean(text_wide * text_wide, -1, keepdims=True) + EPS)
    normed = text_wide * tnorm
    pairs = lax.dynamic_slice_in_dim(pair_image, first_caption, count)
    image_ids = first_image + jnp.arange(keys.shape[0], dtype=jnp.int32)

    def one_image(carry, item):
        keys_one, values_one, image_id = item
        loss, grad_x, grad_k, grad_v = image_terms(
            block_text, normed, tnorm, pairs, image_id, keys_one, values_one
        )
        return ((carry[0] + loss, carry[1] + grad_x), (grad_k, grad_v))

    start = (jnp.zeros((count,), jnp.float32), jnp.zeros((count, width), jnp.float32))
    (loss_sum, grad_text), (grad_keys, grad_values) = lax.scan(
        one_image, start, (keys, values, image_ids)
    )
    return (loss_sum, grad_text, grad_keys, grad_values)


def local(text, keys, values, pair_image):
    per_device = keys.shape[0]
    groups = lax.axis_size("blk")
    members = lax.axis_size("grp")
    group_index = lax.axis_index("blk")
    first_image = (group_index * members + lax.axis_index("grp")) * per_device
    image_total = per_device * groups * members
    group_text = lax.all_gather(text, "grp", axis=0, tiled=True)
    span = group_text.shape[0]
    carried = (jnp.zeros((span,), jnp.float32), jnp.zeros((span, text.shape[1]), jnp.float32))
    grad_keys = jnp.zeros(keys.shape, jnp.float32)
    grad_values = jnp.zeros(values.shape, jnp.float32)
    for turn in range(groups):
        source = (group_index - turn) % groups
        loss_part, grad_part, keys_part, values_part = pair_block(
            group_text, pair_image, source * span, keys, values, first_image
        )
        carried = (carried[0] + loss_part, carried[1] + grad_part)
        grad_keys = grad_keys + keys_part
        grad_values = grad_values + values_part
        if turn + 1 < groups:
            group_text = passed_along(group_text, "blk", 1)
        carried = passed_along((carried[0], carried[1]), "blk", 1)
    loss_own, grad_own = (
        lax.psum_scatter(carried[0], "grp", scatter_dimension=0, tiled=True),
        lax.psum_scatter(carried[1], "grp", scatter_dimension=0, tiled=True),
    )
    return (loss_own / image_total, grad_own, grad_keys, grad_values)


def solution(mesh):
    placed = (
        P(("blk", "grp"), None),
        P(("blk", "grp"), None, None),
        P(("blk", "grp"), None, None),
        P(),
    )
    return jax.shard_map(
        local,
        mesh=mesh,
        in_specs=placed,
        out_specs=(
            P(("blk", "grp")),
            P(("blk", "grp"), None),
            P(("blk", "grp"), None, None),
            P(("blk", "grp"), None, None),
        ),
        check_vma=False,
    )
```

profile of v0, /device:TPU:0, one launch (start us, length us, event | category | flops | bytes accessed | tf_op | source)
XLA Modules:
  0.0 104.7 jit_solution(5783523239401266928)
XLA Ops:
  0.6 28.1 %all-gather = bf16[8,1,512]{2,1,0:T(2,128)(2,1)S(1)} all-gather(bf16[1,1,512]{2,1,0:T(2,128)(2,1)} %bitcast.91), channel_id=1, replica_groups=mesh['blk'=4,'grp'=8] {'grp'}, dimensions={0}, use_global_device_ids=true | all-gather | bytes 9216 | tf_op jit(solution)/shard_map/all_gather | solution.py:92
  28.7 0.1 fusion.102
  28.9 1.1 %copy.92 = bf16[1,196,512]{1,2,0:T(8,128)(2,1)S(1)} copy(bf16[1,196,512]{2,1,0:T(8,128)(2,1)} %param.6) | data formatting | bytes 401408 | tf_op args[2]
  30.0 0.1 copy.90
  30.3 0.1 fusion.31
  30.4 1.3 %fusion.180 = (f32[8,8]{0,1:T(8,128)S(1)}, f32[8,8,196]{2,0,1:T(8,128)S(1)}) fusion(f32[8,8,196]{2,0,1:T(8,128)S(1)} %fusion.31), kind=kOutput, calls=%fused_computation.247 | output fusion | flops 25283 | bytes 100608 | tf_op jit(solution)/shard_map/while/body/eval_jaxpr/sub | solution.py:28
  31.8 0.4 multiply_reduce_fusion.7
  32.3 0.2 fusion.97
  32.5 0.5 copy-done.1
  33.0 1.6 %collective-permute-start = (f32[8]{0:T(128)S(1)}, f32[8]{0:T(128)S(1)}, u32[]{:S(2)}, u32[]{:S(2)}) collective-permute-start(f32[8]{0:T(128)S(1)} %compare_select_fusion.3), channel_id=1, source_target_pairs={{24,0},{0,8},{8,16},{16,24},{25,1},{1,9},{9,17},{17,25},{26,2},{2,... | collective-permute-start | bytes 104 | tf_op jit(solution)/shard_map/ppermute | solution.py:15
  34.7 0.2 fusion.98
  34.9 0.1 reshape.340
  35.0 0.1 convolution_bitcast_fusion.3
  35.2 0.3 convolution_bitcast_fusion.7
  35.7 0.4 fusion.36
  36.1 0.3 fusion.130
  36.6 0.6 copy-done.2
  37.2 0.6 dynamic-slice
  37.9 0.1 fusion.30
  38.0 1.3 %fusion.179 = (f32[8,8]{0,1:T(8,128)S(1)}, f32[8,8,196]{2,0,1:T(8,128)S(1)}) fusion(f32[8,8,196]{2,0,1:T(8,128)S(1)} %fusion.30), kind=kOutput, calls=%fused_computation.246 | output fusion | flops 25283 | bytes 100608 | tf_op jit(solution)/shard_map/while/body/eval_jaxpr/sub | solution.py:28
  39.3 0.4 multiply_reduce_fusion.6
  39.8 0.1 fusion.109
  40.0 0.2 fusion.103
  40.2 0.1 fusion.165
  40.3 0.7 collective-permute-start.2
  40.9 0.2 fusion.104
  41.2 0.1 reshape.342
  41.3 0.1 convolution_bitcast_fusion.2
  41.5 0.3 convolution_bitcast_fusion.6
  41.8 0.4 convolution_add_fusion.5
  42.2 0.3 convolution_add_fusion.2
  42.7 3.0 %collective-permute-done.3 = bf16[8,512]{1,0:T(8,128)(2,1)S(1)} collective-permute-done((bf16[8,512]{1,0:T(8,128)(2,1)S(1)}, bf16[8,512]{1,0:T(8,128)(2,1)S(1)}, u32[]{:S(2)}, u32[]{:S(2)}) %collective-permute-start.3) | collective-permute-done | bytes 8224 | tf_op jit(solution)/shard_map/ppermute | solution.py:15
  45.8 0.1 fusion.29
  45.9 1.3 %fusion.178 = (f32[8,8]{0,1:T(8,128)S(1)}, f32[8,8,196]{2,0,1:T(8,128)S(1)}) fusion(f32[8,8,196]{2,0,1:T(8,128)S(1)} %fusion.29), kind=kOutput, calls=%fused_computation.245 | output fusion | flops 25283 | bytes 100608 | tf_op jit(solution)/shard_map/while/body/eval_jaxpr/sub | solution.py:28
  47.2 0.4 multiply_reduce_fusion.5
  47.7 0.1 fusion.116
  47.9 0.2 fusion.110
  48.1 0.1 fusion.166
  48.3 1.6 %collective-permute-start.8 = (f32[8,512]{1,0:T(8,128)S(1)}, f32[8,512]{1,0:T(8,128)S(1)}, u32[]{:S(2)}, u32[]{:S(2)}) collective-permute-start(f32[8,512]{1,0:T(8,128)S(1)} %fusion.108), channel_id=1, source_target_pairs={{24,0},{0,8},{8,16},{16,24},{25,1},{1,9},{9,17},{17,25},{26,2},{2,... | collective-permute-start | bytes 49160 | tf_op jit(solution)/shard_map/ppermute | solution.py:15
  49.9 0.2 fusion.111
  50.3 0.1 convolution_bitcast_fusion.1
  50.4 0.3 convolution_bitcast_fusion.5
  50.7 0.4 convolution_add_fusion.4
  51.2 0.3 convolution_add_fusion.1
  51.7 3.0 %collective-permute-done.5 = bf16[8,512]{1,0:T(8,128)(2,1)S(1)} collective-permute-done((bf16[8,512]{1,0:T(8,128)(2,1)S(1)}, bf16[8,512]{1,0:T(8,128)(2,1)S(1)}, u32[]{:S(2)}, u32[]{:S(2)}) %collective-permute-start.5) | collective-permute-done | bytes 8224 | tf_op jit(solution)/shard_map/ppermute | solution.py:15
  54.7 0.1 fusion.28
  54.9 1.3 %fusion.177 = (f32[8,8]{0,1:T(8,128)S(1)}, f32[8,8,196]{2,0,1:T(8,128)S(1)}) fusion(f32[8,8,196]{2,0,1:T(8,128)S(1)} %fusion.28), kind=kOutput, calls=%fused_computation.244 | output fusion | flops 25283 | bytes 100608 | tf_op jit(solution)/shard_map/while/body/eval_jaxpr/sub | solution.py:28
  56.2 0.4 multiply_reduce_fusion.4
  56.7 0.1 fusion.123
  56.8 0.2 fusion.117
  57.0 0.1 fusion.167
  57.2 0.2 fusion.118
  57.6 0.1 convolution_bitcast_fusion
  57.7 0.4 convolution_add_fusion.3
  58.1 0.3 convolution_bitcast_fusion.4
  58.5 0.6 collective-permute-start.9
  59.3 2.4 %collective-permute-done.9 = f32[8,512]{1,0:T(8,128)S(1)} collective-permute-done((f32[8,512]{1,0:T(8,128)S(1)}, f32[8,512]{1,0:T(8,128)S(1)}, u32[]{:S(2)}, u32[]{:S(2)}) %collective-permute-start.9) | collective-permute-done | bytes 16416 | tf_op jit(solution)/shard_map/ppermute | solution.py:15
  61.8 0.3 convolution_add_fusion
  62.1 1.0 copy.116
  63.2 1.0 copy.117
  64.2 0.8 collective-permute-done.10
  65.0 35.4 %all-reduce.2 = (f32[8]{0:T(128)S(1)}, f32[8,512]{1,0:T(8,128)S(1)}) all-reduce(f32[8]{0:T(128)S(1)} %collective-permute-done.6, f32[8,512]{1,0:T(8,128)S(1)} %collective-permute-done.10), channel_id=2, replica_groups=mesh['blk'=4,'grp'=8] {'grp'}, use_global_device_ids=true, to_apply=%region_20.21.clone | all-reduce | flops 4104 | bytes 32832
  100.4 1.3 %dynamic-slice.1 = f32[1]{0:T(128)} dynamic-slice(f32[8]{0:T(128)S(1)} %get-tuple-element.148, u32[]{:T(128)} %bitcast.23), dynamic_slice_sizes={1} | dynamic-slice | bytes 12
  101.7 1.2 %constant_dynamic-slice_fusion = f32[1,512]{1,0:T(1,128)} fusion(f32[8,512]{1,0:T(8,128)S(1)} %get-tuple-element.149, u32[]{:T(128)} %bitcast.23), kind=kLoop, calls=%fused_computation.211 | loop fusion | bytes 4100
  (65 shorter events, 2.5 us)
Async XLA Ops:
  28.8 9.0 %collective-permute-start.1 = (bf16[8,512]{1,0:T(8,128)(2,1)S(1)}, bf16[8,512]{1,0:T(8,128)(2,1)S(1)}, u32[]{:S(2)}, u32[]{:S(2)}) collective-permute-start(bf16[8,512]{1,0:T(8,128)(2,1)S(1)} %get-tuple-element.153), channel_id=1, source_target_pairs={{24,0},{0,8},{8,16},{16,24},{25,1},{1,9},{9,17},{17,25},{26,2},{2,... | collective-permute-start | bytes 24584 | tf_op jit(solution)/shard_map/ppermute | solution.py:15
  28.9 1.1 %copy-start = (bf16[1,196,512]{2,1,0:T(8,128)(2,1)S(1)}, bf16[1,196,512]{2,1,0:T(8,128)(2,1)}, u32[]{:S(2)}) copy-start(bf16[1,196,512]{2,1,0:T(8,128)(2,1)} %param.5) | copy-start | bytes 602116
  32.3 0.7 copy-start.1
  33.0 7.1 %collective-permute-start = (f32[8]{0:T(128)S(1)}, f32[8]{0:T(128)S(1)}, u32[]{:S(2)}, u32[]{:S(2)}) collective-permute-start(f32[8]{0:T(128)S(1)} %compare_select_fusion.3), channel_id=1, source_target_pairs={{24,0},{0,8},{8,16},{16,24},{25,1},{1,9},{9,17},{17,25},{26,2},{2,... | collective-permute-start | bytes 104 | tf_op jit(solution)/shard_map/ppermute | solution.py:15
  35.7 12.5 %collective-permute-start.7 = (f32[8,512]{1,0:T(8,128)S(1)}, f32[8,512]{1,0:T(8,128)S(1)}, u32[]{:S(2)}, u32[]{:S(2)}) collective-permute-start(f32[8,512]{1,0:T(8,128)S(1)} %fusion.101), channel_id=1, source_target_pairs={{24,0},{0,8},{8,16},{16,24},{25,1},{1,9},{9,17},{17,25},{26,2},{2,... | collective-permute-start | bytes 49160 | tf_op jit(solution)/shard_map/ppermute | solution.py:15
  36.6 0.7 copy-start.2
  40.3 7.8 %collective-permute-start.2 = (f32[8]{0:T(128)S(1)}, f32[8]{0:T(128)S(1)}, u32[]{:S(2)}, u32[]{:S(2)}) collective-permute-start(f32[8]{0:T(128)S(1)} %get-tuple-element.171), channel_id=1, source_target_pairs={{24,0},{0,8},{8,16},{16,24},{25,1},{1,9},{9,17},{17,25},{26,2},{2,... | collective-permute-start | bytes 104 | tf_op jit(solution)/shard_map/ppermute | solution.py:15
  42.6 3.1 %collective-permute-start.3 = (bf16[8,512]{1,0:T(8,128)(2,1)S(1)}, bf16[8,512]{1,0:T(8,128)(2,1)S(1)}, u32[]{:S(2)}, u32[]{:S(2)}) collective-permute-start(bf16[8,512]{1,0:T(8,128)(2,1)S(1)} %collective-permute-done.1), channel_id=1, source_target_pairs={{24,0},{0,8},{8,16},{16,24},{25,1},{1,9},{9,17},{17,25},{26,2},{2,... | collective-permute-start | bytes 24584 | tf_op jit(solution)/shard_map/ppermute | solution.py:15
  48.2 8.9 %collective-permute-start.4 = (f32[8]{0:T(128)S(1)}, f32[8]{0:T(128)S(1)}, u32[]{:S(2)}, u32[]{:S(2)}) collective-permute-start(f32[8]{0:T(128)S(1)} %get-tuple-element.169), channel_id=1, source_target_pairs={{24,0},{0,8},{8,16},{16,24},{25,1},{1,9},{9,17},{17,25},{26,2},{2,... | collective-permute-start | bytes 104 | tf_op jit(solution)/shard_map/ppermute | solution.py:15
  48.3 10.1 %collective-permute-start.8 = (f32[8,512]{1,0:T(8,128)S(1)}, f32[8,512]{1,0:T(8,128)S(1)}, u32[]{:S(2)}, u32[]{:S(2)}) collective-permute-start(f32[8,512]{1,0:T(8,128)S(1)} %fusion.108), channel_id=1, source_target_pairs={{24,0},{0,8},{8,16},{16,24},{25,1},{1,9},{9,17},{17,25},{26,2},{2,... | collective-permute-start | bytes 49160 | tf_op jit(solution)/shard_map/ppermute | solution.py:15
  51.5 3.1 %collective-permute-start.5 = (bf16[8,512]{1,0:T(8,128)(2,1)S(1)}, bf16[8,512]{1,0:T(8,128)(2,1)S(1)}, u32[]{:S(2)}, u32[]{:S(2)}) collective-permute-start(bf16[8,512]{1,0:T(8,128)(2,1)S(1)} %collective-permute-done.3), channel_id=1, source_target_pairs={{24,0},{0,8},{8,16},{16,24},{25,1},{1,9},{9,17},{17,25},{26,2},{2,... | collective-permute-start | bytes 24584 | tf_op jit(solution)/shard_map/ppermute | solution.py:15
  57.1 7.0 %collective-permute-start.6 = (f32[8]{0:T(128)S(1)}, f32[8]{0:T(128)S(1)}, u32[]{:S(2)}, u32[]{:S(2)}) collective-permute-start(f32[8]{0:T(128)S(1)} %get-tuple-element.155), channel_id=1, source_target_pairs={{24,0},{0,8},{8,16},{16,24},{25,1},{1,9},{9,17},{17,25},{26,2},{2,... | collective-permute-start | bytes 104 | tf_op jit(solution)/shard_map/ppermute | solution.py:15
  58.5 3.2 %collective-permute-start.9 = (f32[8,512]{1,0:T(8,128)S(1)}, f32[8,512]{1,0:T(8,128)S(1)}, u32[]{:S(2)}, u32[]{:S(2)}) collective-permute-start(f32[8,512]{1,0:T(8,128)S(1)} %fusion.115), channel_id=1, source_target_pairs={{24,0},{0,8},{8,16},{16,24},{25,1},{1,9},{9,17},{17,25},{26,2},{2,... | collective-permute-start | bytes 49160 | tf_op jit(solution)/shard_map/ppermute | solution.py:15
  61.8 3.2 %collective-permute-start.10 = (f32[8,512]{1,0:T(8,128)S(1)}, f32[8,512]{1,0:T(8,128)S(1)}, u32[]{:S(2)}, u32[]{:S(2)}) collective-permute-start(f32[8,512]{1,0:T(8,128)S(1)} %fusion.122), channel_id=1, source_target_pairs={{24,0},{0,8},{8,16},{16,24},{25,1},{1,9},{9,17},{17,25},{26,2},{2,... | collective-permute-start | bytes 49160 | tf_op jit(solution)/shard_map/ppermute | solution.py:15
where the time goes:
time: 105 us
  blocking collectives  63.5 us (60%)
  waiting for transfers between devices  9.17 us (9%)
  local copies, waits for them, and re-layouts  8.86 us (8%)
  other arithmetic  8.36 us (8%)
  matrix products  7.13 us (7%)
  starting transfers between devices  4.88 us (5%)
  between operations  2.85 us (3%)
    unnamed x1, blocking collectives  35.4 us
    all_gather x1, blocking collectives, local(): group_text = lax.all_gather(text, 'grp', axis=0, tiled=True)  28.1 us
    ppermute x11, waiting for transfers between devices, passed_along(): return lax.ppermute(block, axis, route)  9.17 us
    unnamed x13, local copies, waits for them, and re-layouts  7.48 us
    sub x4, other arithmetic, image_terms(): weights = jax.nn.softmax(scores, axis=-1)  5.22 us
    ppermute x11, starting transfers between devices, passed_along(): return lax.ppermute(block, axis, route)  4.88 us
  transfers between devices with their start and end apart: 11, of which 4 were waited for; matrix products, arithmetic and copies ran while one was open for 20% of the time, Pallas kernels for 0%

commit v1 on v0

--- a/solution.py
+++ b/solution.py
@@ -89,7 +89,12 @@
     group_index = lax.axis_index("blk")
     first_image = (group_index * members + lax.axis_index("grp")) * per_device
     image_total = per_device * groups * members
-    group_text = lax.all_gather(text, "grp", axis=0, tiled=True)
+    ring = [text]
+    for hop in range(7):
+        ring.append(lax.ppermute(ring[-1], "grp", [(dev, (dev + 1) % 8) for dev in range(8)]))
+    group_text = jnp.roll(
+        jnp.concatenate(ring[::-1], axis=0), (lax.axis_index("grp") + 1) * ring[0].shape[0], axis=0
+    )
     span = group_text.shape[0]
     carried = (jnp.zeros((span,), jnp.float32), jnp.zeros((span, text.shape[1]), jnp.float32))
     grad_keys = jnp.zeros(keys.shape, jnp.float32)

time: 105 us -> 117 us (1.11)
  waiting for transfers between devices: 9.17 us -> 44.5 us
  blocking collectives: 63.5 us -> 33.9 us
  starting transfers between devices: 4.88 us -> 10.9 us
    ppermute x0 -> x7, waiting for transfers between devices: none -> 39.9 us  [local(): lax.ppermute(ring[-1], 'grp', [(dev, (dev + 1) % 8) for dev in range(8)])]
    all_gather x1 -> x0, blocking collectives: 28.1 us -> none  [local(): group_text = lax.all_gather(text, 'grp', axis=0, tiled=True)]
    ppermute x11, waiting for transfers between devices: 9.17 us -> 4.61 us  [passed_along(): return lax.ppermute(block, axis, route)]
    ppermute x0 -> x7, starting transfers between devices: none -> 3.06 us  [local(): lax.ppermute(ring[-1], 'grp', [(dev, (dev + 1) % 8) for dev in range(8)])]
    ppermute x11, starting transfers between devices: 4.88 us -> 7.82 us  [passed_along(): return lax.ppermute(block, axis, route)]
    unnamed x1, blocking collectives: 35.4 us -> 33.9 us
    unnamed x13 -> x15, local copies, waits for them, and re-layouts: 7.48 us -> 7.49 us
  transfers between devices with their start and end apart: 11 -> 18, of which waited for: 4 -> 11; matrix products, arithmetic and copies ran while one was open for 20% -> 18% of each run, Pallas kernels for 0% -> 0%
where the time goes in v1:
time: 117 us
  waiting for transfers between devices  44.5 us (38%)
  blocking collectives  33.9 us (29%)
  starting transfers between devices  10.9 us (9%)
  local copies, waits for them, and re-layouts  8.94 us (8%)
  other arithmetic  8.34 us (7%)
  matrix products  7.12 us (6%)
  between operations  2.81 us (2%)
    ppermute x7, waiting for transfers between devices, local(): lax.ppermute(ring[-1], 'grp', [(dev, (dev + 1) % 8) for dev in range(8)])  39.9 us
    unnamed x1, blocking collectives  33.9 us
    ppermute x11, starting transfers between devices, passed_along(): return lax.ppermute(block, axis, route)  7.82 us
    unnamed x15, local copies, waits for them, and re-layouts  7.49 us
    sub x4, other arithmetic, image_terms(): weights = jax.nn.softmax(scores, axis=-1)  5.22 us
    ppermute x11, waiting for transfers between devices, passed_along(): return lax.ppermute(block, axis, route)  4.61 us
    ppermute x7, starting transfers between devices, local(): lax.ppermute(ring[-1], 'grp', [(dev, (dev + 1) % 8) for dev in range(8)])  3.06 us
  transfers between devices with their start and end apart: 18, of which 11 were waited for; matrix products, arithmetic and copies ran while one was open for 18% of the time, Pallas kernels for 0%

profile of v1, /device:TPU:0, one launch (start us, length us, event | category | flops | bytes accessed | tf_op | source)
XLA Modules:
  0.0 116.5 jit_solution(6766127199659232967)
XLA Ops:
  0.6 3.0 %collective-permute-start = (bf16[1,512]{1,0:T(2,128)(2,1)}, bf16[1,512]{1,0:T(2,128)(2,1)S(1)}, u32[]{:S(2)}, u32[]{:S(2)}) collective-permute-start(bf16[1,512]{1,0:T(2,128)(2,1)} %param.4), channel_id=1, source_target_pairs={{0,1},{1,2},{2,3},{3,4},{4,5},{5,6},{6,7},{7,0},{8,9},{9,10},{10,1... | collective-permute-start | bytes 3080 | tf_op jit(solution)/shard_map/ppermute | solution.py:94
  3.7 4.8 %collective-permute-done = bf16[1,512]{1,0:T(2,128)(2,1)S(1)} collective-permute-done((bf16[1,512]{1,0:T(2,128)(2,1)}, bf16[1,512]{1,0:T(2,128)(2,1)S(1)}, u32[]{:S(2)}, u32[]{:S(2)}) %collective-permute-start) | collective-permute-done | bytes 1056 | tf_op jit(solution)/shard_map/ppermute | solution.py:94
  8.5 6.3 %collective-permute-done.1 = bf16[1,512]{1,0:T(2,128)(2,1)S(1)} collective-permute-done((bf16[1,512]{1,0:T(2,128)(2,1)S(1)}, bf16[1,512]{1,0:T(2,128)(2,1)S(1)}, u32[]{:S(2)}, u32[]{:S(2)}) %collective-permute-start.1) | collective-permute-done | bytes 1056 | tf_op jit(solution)/shard_map/ppermute | solution.py:94
  14.8 6.3 %collective-permute-done.2 = bf16[1,512]{1,0:T(2,128)(2,1)S(1)} collective-permute-done((bf16[1,512]{1,0:T(2,128)(2,1)S(1)}, bf16[1,512]{1,0:T(2,128)(2,1)S(1)}, u32[]{:S(2)}, u32[]{:S(2)}) %collective-permute-start.2) | collective-permute-done | bytes 1056 | tf_op jit(solution)/shard_map/ppermute | solution.py:94
  21.1 6.3 %collective-permute-done.3 = bf16[1,512]{1,0:T(2,128)(2,1)S(1)} collective-permute-done((bf16[1,512]{1,0:T(2,128)(2,1)S(1)}, bf16[1,512]{1,0:T(2,128)(2,1)S(1)}, u32[]{:S(2)}, u32[]{:S(2)}) %collective-permute-start.3) | collective-permute-done | bytes 1056 | tf_op jit(solution)/shard_map/ppermute | solution.py:94
  27.3 6.3 %collective-permute-done.4 = bf16[1,512]{1,0:T(2,128)(2,1)S(1)} collective-permute-done((bf16[1,512]{1,0:T(2,128)(2,1)S(1)}, bf16[1,512]{1,0:T(2,128)(2,1)S(1)}, u32[]{:S(2)}, u32[]{:S(2)}) %collective-permute-start.4) | collective-permute-done | bytes 1056 | tf_op jit(solution)/shard_map/ppermute | solution.py:94
  33.6 6.3 %collective-permute-done.5 = bf16[1,512]{1,0:T(2,128)(2,1)S(1)} collective-permute-done((bf16[1,512]{1,0:T(2,128)(2,1)S(1)}, bf16[1,512]{1,0:T(2,128)(2,1)S(1)}, u32[]{:S(2)}, u32[]{:S(2)}) %collective-permute-start.5) | collective-permute-done | bytes 1056 | tf_op jit(solution)/shard_map/ppermute | solution.py:94
  39.9 1.1 copy.73
  41.0 0.1 copy.70
  41.2 0.6 copy-done.3
  41.9 0.6 dynamic-slice
  42.5 3.7 %collective-permute-done.6 = bf16[1,512]{1,0:T(2,128)(2,1)S(1)} collective-permute-done((bf16[1,512]{1,0:T(2,128)(2,1)S(1)}, bf16[1,512]{1,0:T(2,128)(2,1)S(1)}, u32[]{:S(2)}, u32[]{:S(2)}) %collective-permute-start.6) | collective-permute-done | bytes 1056 | tf_op jit(solution)/shard_map/ppermute | solution.py:94
  46.3 0.1 fusion.102
  46.5 0.1 fusion.31
  46.7 1.3 %fusion.180 = (f32[8,8]{0,1:T(8,128)S(1)}, f32[8,8,196]{2,0,1:T(8,128)S(1)}) fusion(f32[8,8,196]{2,0,1:T(8,128)S(1)} %fusion.31), kind=kOutput, calls=%fused_computation.247 | output fusion | flops 25283 | bytes 100608 | tf_op jit(solution)/shard_map/while/body/eval_jaxpr/sub | solution.py:28
  48.0 0.4 multiply_reduce_fusion.7
  48.5 0.2 fusion.97
  48.7 0.5 copy-done.2
  49.2 0.2 fusion.98
  49.6 0.1 convolution_bitcast_fusion.3
  49.8 0.3 fusion.130
  50.2 1.8 %collective-permute-start.7 = (f32[8]{0:T(128)S(1)}, f32[8]{0:T(128)S(1)}, u32[]{:S(2)}, u32[]{:S(2)}) collective-permute-start(f32[8]{0:T(128)S(1)} %compare_select_fusion.3), channel_id=1, source_target_pairs={{24,0},{0,8},{8,16},{16,24},{25,1},{1,9},{9,17},{17,25},{26,2},{2,... | collective-permute-start | bytes 104 | tf_op jit(solution)/shard_map/ppermute | solution.py:15
  52.0 0.3 convolution_bitcast_fusion.7
  52.6 0.1 fusion.30
  52.7 1.3 %fusion.179 = (f32[8,8]{0,1:T(8,128)S(1)}, f32[8,8,196]{2,0,1:T(8,128)S(1)}) fusion(f32[8,8,196]{2,0,1:T(8,128)S(1)} %fusion.30), kind=kOutput, calls=%fused_computation.246 | output fusion | flops 25283 | bytes 100608 | tf_op jit(solution)/shard_map/while/body/eval_jaxpr/sub | solution.py:28
  54.0 0.4 multiply_reduce_fusion.6
  54.6 0.2 fusion.103
  54.9 0.2 fusion.104
  55.3 0.1 convolution_bitcast_fusion.2
  55.5 0.3 convolution_bitcast_fusion.6
  55.8 0.4 fusion.36
  56.2 0.5 collective-permute-start.9
  56.7 0.4 convolution_add_fusion.5
  57.2 0.3 convolution_add_fusion.2
  57.7 1.7 %collective-permute-start.15 = (f32[8,512]{1,0:T(8,128)S(1)}, f32[8,512]{1,0:T(8,128)S(1)}, u32[]{:S(2)}, u32[]{:S(2)}) collective-permute-start(f32[8,512]{1,0:T(8,128)S(1)} %fusion.108), channel_id=1, source_target_pairs={{24,0},{0,8},{8,16},{16,24},{25,1},{1,9},{9,17},{17,25},{26,2},{2,... | collective-permute-start | bytes 49160 | tf_op jit(solution)/shard_map/ppermute | solution.py:15
  59.5 1.2 %collective-permute-done.10 = bf16[8,512]{1,0:T(8,128)(2,1)S(1)} collective-permute-done((bf16[8,512]{1,0:T(8,128)(2,1)S(1)}, bf16[8,512]{1,0:T(8,128)(2,1)S(1)}, u32[]{:S(2)}, u32[]{:S(2)}) %collective-permute-start.10) | collective-permute-done | bytes 8224 | tf_op jit(solution)/shard_map/ppermute | solution.py:15
  60.8 0.1 fusion.29
  60.9 1.3 %fusion.178 = (f32[8,8]{0,1:T(8,128)S(1)}, f32[8,8,196]{2,0,1:T(8,128)S(1)}) fusion(f32[8,8,196]{2,0,1:T(8,128)S(1)} %fusion.29), kind=kOutput, calls=%fused_computation.245 | output fusion | flops 25283 | bytes 100608 | tf_op jit(solution)/shard_map/while/body/eval_jaxpr/sub | solution.py:28
  62.2 0.4 multiply_reduce_fusion.5
  62.9 0.2 fusion.110
  63.2 0.2 fusion.111
  63.6 0.1 convolution_bitcast_fusion.1
  63.7 0.3 convolution_bitcast_fusion.5
  64.1 0.4 convolution_add_fusion.4
  64.5 0.3 convolution_add_fusion.1
  64.9 1.8 %collective-permute-start.12 = (bf16[8,512]{1,0:T(8,128)(2,1)S(1)}, bf16[8,512]{1,0:T(8,128)(2,1)S(1)}, u32[]{:S(2)}, u32[]{:S(2)}) collective-permute-start(bf16[8,512]{1,0:T(8,128)(2,1)S(1)} %collective-permute-done.10), channel_id=1, source_target_pairs={{24,0},{0,8},{8,16},{16,24},{25,1},{1,9},{9,17},{17,25},{26,2},{2,... | collective-permute-start | bytes 24584 | tf_op jit(solution)/shard_map/ppermute | solution.py:15
  66.7 1.2 %collective-permute-done.12 = bf16[8,512]{1,0:T(8,128)(2,1)S(1)} collective-permute-done((bf16[8,512]{1,0:T(8,128)(2,1)S(1)}, bf16[8,512]{1,0:T(8,128)(2,1)S(1)}, u32[]{:S(2)}, u32[]{:S(2)}) %collective-permute-start.12) | collective-permute-done | bytes 8224 | tf_op jit(solution)/shard_map/ppermute | solution.py:15
  68.1 0.1 fusion.28
  68.2 1.3 %fusion.177 = (f32[8,8]{0,1:T(8,128)S(1)}, f32[8,8,196]{2,0,1:T(8,128)S(1)}) fusion(f32[8,8,196]{2,0,1:T(8,128)S(1)} %fusion.28), kind=kOutput, calls=%fused_computation.244 | output fusion | flops 25283 | bytes 100608 | tf_op jit(solution)/shard_map/while/body/eval_jaxpr/sub | solution.py:28
  69.5 0.4 multiply_reduce_fusion.4
  70.1 0.2 fusion.117
  70.5 0.2 fusion.118
  70.9 0.1 convolution_bitcast_fusion
  71.0 0.4 convolution_add_fusion.3
  71.5 0.3 convolution_bitcast_fusion.4
  71.9 1.8 %collective-permute-start.16 = (f32[8,512]{1,0:T(8,128)S(1)}, f32[8,512]{1,0:T(8,128)S(1)}, u32[]{:S(2)}, u32[]{:S(2)}) collective-permute-start(f32[8,512]{1,0:T(8,128)S(1)} %fusion.115), channel_id=1, source_target_pairs={{24,0},{0,8},{8,16},{16,24},{25,1},{1,9},{9,17},{17,25},{26,2},{2,... | collective-permute-start | bytes 49160 | tf_op jit(solution)/shard_map/ppermute | solution.py:15
  73.7 1.3 %collective-permute-done.16 = f32[8,512]{1,0:T(8,128)S(1)} collective-permute-done((f32[8,512]{1,0:T(8,128)S(1)}, f32[8,512]{1,0:T(8,128)S(1)}, u32[]{:S(2)}, u32[]{:S(2)}) %collective-permute-start.16) | collective-permute-done | bytes 16416 | tf_op jit(solution)/shard_map/ppermute | solution.py:15
  75.1 0.3 convolution_add_fusion
  75.5 1.0 copy.100
  76.5 1.0 copy.101
  77.5 0.8 collective-permute-done.17
  78.3 33.9 %all-reduce.2 = (f32[8]{0:T(128)S(1)}, f32[8,512]{1,0:T(8,128)S(1)}) all-reduce(f32[8]{0:T(128)S(1)} %collective-permute-done.13, f32[8,512]{1,0:T(8,128)S(1)} %collective-permute-done.17), channel_id=2, replica_groups=mesh['blk'=4,'grp'=8] {'grp'}, use_global_device_ids=true, to_apply=%region_20.21.clone | all-reduce | flops 4104 | bytes 32832
  112.2 1.3 %dynamic-slice.1 = f32[1]{0:T(128)} dynamic-slice(f32[8]{0:T(128)S(1)} %get-tuple-element.144, u32[]{:T(128)} %bitcast.22), dynamic_slice_sizes={1} | dynamic-slice | bytes 12
  113.5 1.2 %constant_dynamic-slice_fusion = f32[1,512]{1,0:T(1,128)} fusion(f32[8,512]{1,0:T(8,128)S(1)} %get-tuple-element.145, u32[]{:T(128)} %bitcast.22), kind=kLoop, calls=%fused_computation.210 | loop fusion | bytes 4100
  (80 shorter events, 3.2 us)
Async XLA Ops:
  0.6 7.9 %collective-permute-start = (bf16[1,512]{1,0:T(2,128)(2,1)}, bf16[1,512]{1,0:T(2,128)(2,1)S(1)}, u32[]{:S(2)}, u32[]{:S(2)}) collective-permute-start(bf16[1,512]{1,0:T(2,128)(2,1)} %param.4), channel_id=1, source_target_pairs={{0,1},{1,2},{2,3},{3,4},{4,5},{5,6},{6,7},{7,0},{8,9},{9,10},{10,1... | collective-permute-start | bytes 3080 | tf_op jit(solution)/shard_map/ppermute | solution.py:94
  8.5 6.3 %collective-permute-start.1 = (bf16[1,512]{1,0:T(2,128)(2,1)S(1)}, bf16[1,512]{1,0:T(2,128)(2,1)S(1)}, u32[]{:S(2)}, u32[]{:S(2)}) collective-permute-start(bf16[1,512]{1,0:T(2,128)(2,1)S(1)} %collective-permute-done), channel_id=1, source_target_pairs={{0,1},{1,2},{2,3},{3,4},{4,5},{5,6},{6,7},{7,0},{8,9},{9,10},{10,1... | collective-permute-start | bytes 3080 | tf_op jit(solution)/shard_map/ppermute | solution.py:94
  14.8 6.3 %collective-permute-start.2 = (bf16[1,512]{1,0:T(2,128)(2,1)S(1)}, bf16[1,512]{1,0:T(2,128)(2,1)S(1)}, u32[]{:S(2)}, u32[]{:S(2)}) collective-permute-start(bf16[1,512]{1,0:T(2,128)(2,1)S(1)} %collective-permute-done.1), channel_id=1, source_target_pairs={{0,1},{1,2},{2,3},{3,4},{4,5},{5,6},{6,7},{7,0},{8,9},{9,10},{10,1... | collective-permute-start | bytes 3080 | tf_op jit(solution)/shard_map/ppermute | solution.py:94
  21.1 6.3 %collective-permute-start.3 = (bf16[1,512]{1,0:T(2,128)(2,1)S(1)}, bf16[1,512]{1,0:T(2,128)(2,1)S(1)}, u32[]{:S(2)}, u32[]{:S(2)}) collective-permute-start(bf16[1,512]{1,0:T(2,128)(2,1)S(1)} %collective-permute-done.2), channel_id=1, source_target_pairs={{0,1},{1,2},{2,3},{3,4},{4,5},{5,6},{6,7},{7,0},{8,9},{9,10},{10,1... | collective-permute-start | bytes 3080 | tf_op jit(solution)/shard_map/ppermute | solution.py:94
  27.3 6.3 %collective-permute-start.4 = (bf16[1,512]{1,0:T(2,128)(2,1)S(1)}, bf16[1,512]{1,0:T(2,128)(2,1)S(1)}, u32[]{:S(2)}, u32[]{:S(2)}) collective-permute-start(bf16[1,512]{1,0:T(2,128)(2,1)S(1)} %collective-permute-done.3), channel_id=1, source_target_pairs={{0,1},{1,2},{2,3},{3,4},{4,5},{5,6},{6,7},{7,0},{8,9},{9,10},{10,1... | collective-permute-start | bytes 3080 | tf_op jit(solution)/shard_map/ppermute | solution.py:94
  33.6 6.3 %collective-permute-start.5 = (bf16[1,512]{1,0:T(2,128)(2,1)S(1)}, bf16[1,512]{1,0:T(2,128)(2,1)S(1)}, u32[]{:S(2)}, u32[]{:S(2)}) collective-permute-start(bf16[1,512]{1,0:T(2,128)(2,1)S(1)} %collective-permute-done.4), channel_id=1, source_target_pairs={{0,1},{1,2},{2,3},{3,4},{4,5},{5,6},{6,7},{7,0},{8,9},{9,10},{10,1... | collective-permute-start | bytes 3080 | tf_op jit(solution)/shard_map/ppermute | solution.py:94
  39.9 6.3 %collective-permute-start.6 = (bf16[1,512]{1,0:T(2,128)(2,1)S(1)}, bf16[1,512]{1,0:T(2,128)(2,1)S(1)}, u32[]{:S(2)}, u32[]{:S(2)}) collective-permute-start(bf16[1,512]{1,0:T(2,128)(2,1)S(1)} %collective-permute-done.5), channel_id=1, source_target_pairs={{0,1},{1,2},{2,3},{3,4},{4,5},{5,6},{6,7},{7,0},{8,9},{9,10},{10,1... | collective-permute-start | bytes 3080 | tf_op jit(solution)/shard_map/ppermute | solution.py:94
  39.9 1.1 copy-start
  41.2 5.0 %copy-start.1 = (bf16[1,512]{1,0:T(2,128)(2,1)S(1)}, bf16[1,512]{1,0:T(2,128)(2,1)}, u32[]{:S(2)}) copy-start(bf16[1,512]{1,0:T(2,128)(2,1)} %param.4) | copy-start | bytes 3076
  41.2 0.7 copy-start.3
  46.4 6.1 %collective-permute-start.8 = (bf16[8,512]{1,0:T(8,128)(2,1)S(1)}, bf16[8,512]{1,0:T(8,128)(2,1)S(1)}, u32[]{:S(2)}, u32[]{:S(2)}) collective-permute-start(bf16[8,512]{1,0:T(8,128)(2,1)S(1)} %get-tuple-element.149), channel_id=1, source_target_pairs={{24,0},{0,8},{8,16},{16,24},{25,1},{1,9},{9,17},{17,25},{26,2},{2,... | collective-permute-start | bytes 24584 | tf_op jit(solution)/shard_map/ppermute | solution.py:15
  48.5 0.7 copy-start.2
  50.2 4.7 %collective-permute-start.7 = (f32[8]{0:T(128)S(1)}, f32[8]{0:T(128)S(1)}, u32[]{:S(2)}, u32[]{:S(2)}) collective-permute-start(f32[8]{0:T(128)S(1)} %compare_select_fusion.3), channel_id=1, source_target_pairs={{24,0},{0,8},{8,16},{16,24},{25,1},{1,9},{9,17},{17,25},{26,2},{2,... | collective-permute-start | bytes 104 | tf_op jit(solution)/shard_map/ppermute | solution.py:15
  52.4 5.2 %collective-permute-start.14 = (f32[8,512]{1,0:T(8,128)S(1)}, f32[8,512]{1,0:T(8,128)S(1)}, u32[]{:S(2)}, u32[]{:S(2)}) collective-permute-start(f32[8,512]{1,0:T(8,128)S(1)} %fusion.101), channel_id=1, source_target_pairs={{24,0},{0,8},{8,16},{16,24},{25,1},{1,9},{9,17},{17,25},{26,2},{2,... | collective-permute-start | bytes 49160 | tf_op jit(solution)/shard_map/ppermute | solution.py:15
  56.2 6.8 %collective-permute-start.9 = (f32[8]{0:T(128)S(1)}, f32[8]{0:T(128)S(1)}, u32[]{:S(2)}, u32[]{:S(2)}) collective-permute-start(f32[8]{0:T(128)S(1)} %get-tuple-element.155), channel_id=1, source_target_pairs={{24,0},{0,8},{8,16},{16,24},{25,1},{1,9},{9,17},{17,25},{26,2},{2,... | collective-permute-start | bytes 104 | tf_op jit(solution)/shard_map/ppermute | solution.py:15
  57.6 3.1 %collective-permute-start.10 = (bf16[8,512]{1,0:T(8,128)(2,1)S(1)}, bf16[8,512]{1,0:T(8,128)(2,1)S(1)}, u32[]{:S(2)}, u32[]{:S(2)}) collective-permute-start(bf16[8,512]{1,0:T(8,128)(2,1)S(1)} %collective-permute-done.8), channel_id=1, source_target_pairs={{24,0},{0,8},{8,16},{16,24},{25,1},{1,9},{9,17},{17,25},{26,2},{2,... | collective-permute-start | bytes 24584 | tf_op jit(solution)/shard_map/ppermute | solution.py:15
  57.7 14.1 %collective-permute-start.15 = (f32[8,512]{1,0:T(8,128)S(1)}, f32[8,512]{1,0:T(8,128)S(1)}, u32[]{:S(2)}, u32[]{:S(2)}) collective-permute-start(f32[8,512]{1,0:T(8,128)S(1)} %fusion.108), channel_id=1, source_target_pairs={{24,0},{0,8},{8,16},{16,24},{25,1},{1,9},{9,17},{17,25},{26,2},{2,... | collective-permute-start | bytes 49160 | tf_op jit(solution)/shard_map/ppermute | solution.py:15
  63.2 7.2 %collective-permute-start.11 = (f32[8]{0:T(128)S(1)}, f32[8]{0:T(128)S(1)}, u32[]{:S(2)}, u32[]{:S(2)}) collective-permute-start(f32[8]{0:T(128)S(1)} %get-tuple-element.153), channel_id=1, source_target_pairs={{24,0},{0,8},{8,16},{16,24},{25,1},{1,9},{9,17},{17,25},{26,2},{2,... | collective-permute-start | bytes 104 | tf_op jit(solution)/shard_map/ppermute | solution.py:15
  64.9 3.1 %collective-permute-start.12 = (bf16[8,512]{1,0:T(8,128)(2,1)S(1)}, bf16[8,512]{1,0:T(8,128)(2,1)S(1)}, u32[]{:S(2)}, u32[]{:S(2)}) collective-permute-start(bf16[8,512]{1,0:T(8,128)(2,1)S(1)} %collective-permute-done.10), channel_id=1, source_target_pairs={{24,0},{0,8},{8,16},{16,24},{25,1},{1,9},{9,17},{17,25},{26,2},{2,... | collective-permute-start | bytes 24584 | tf_op jit(solution)/shard_map/ppermute | solution.py:15
  70.4 7.0 %collective-permute-start.13 = (f32[8]{0:T(128)S(1)}, f32[8]{0:T(128)S(1)}, u32[]{:S(2)}, u32[]{:S(2)}) collective-permute-start(f32[8]{0:T(128)S(1)} %get-tuple-element.151), channel_id=1, source_target_pairs={{24,0},{0,8},{8,16},{16,24},{25,1},{1,9},{9,17},{17,25},{26,2},{2,... | collective-permute-start | bytes 104 | tf_op jit(solution)/shard_map/ppermute | solution.py:15
  71.9 3.2 %collective-permute-start.16 = (f32[8,512]{1,0:T(8,128)S(1)}, f32[8,512]{1,0:T(8,128)S(1)}, u32[]{:S(2)}, u32[]{:S(2)}) collective-permute-start(f32[8,512]{1,0:T(8,128)S(1)} %fusion.115), channel_id=1, source_target_pairs={{24,0},{0,8},{8,16},{16,24},{25,1},{1,9},{9,17},{17,25},{26,2},{2,... | collective-permute-start | bytes 49160 | tf_op jit(solution)/shard_map/ppermute | solution.py:15
  75.1 3.2 %collective-permute-start.17 = (f32[8,512]{1,0:T(8,128)S(1)}, f32[8,512]{1,0:T(8,128)S(1)}, u32[]{:S(2)}, u32[]{:S(2)}) collective-permute-start(f32[8,512]{1,0:T(8,128)S(1)} %fusion.122), channel_id=1, source_target_pairs={{24,0},{0,8},{8,16},{16,24},{25,1},{1,9},{9,17},{17,25},{26,2},{2,... | collective-permute-start | bytes 49160 | tf_op jit(solution)/shard_map/ppermute | solution.py:15
